TPU v7x, 512 devices: a whole 4x8x8 slice. The times are simulated.
512 devices in a mesh: seq: 128 (over y, z, core), head: 4 (over x).
Axes of the slice: x: 4, y: 8, z: 8, core: 2. Of those that a mesh axis runs over, the one named last changes fastest.
Arguments:
- queries: bfloat16 [16384, 1536], P('seq', 'head'), may hold values from -400 to 400
- latent: bfloat16 [16384, 320], P(('seq', 'head')), may hold values from -6 to 6
- w_kv_up: bfloat16 [256, 2048], P(None, 'head'), may hold values from -0.375 to 0.375
Outputs:
- attended: bfloat16 [16384, 1024], P('seq', 'head')
All inputs are finite; a program needn't handle non-finite values.
Results may differ from a plain program's by a relative error of at most 0.004.
Values may be sent and summed in bfloat16 or wider, within the bound.
No kernel may reach another device: no remote copies, remote signals or barrier semaphores. Data moves between devices by JAX's collectives and lax.ppermute only.
A program may use at most 64 MiB of HBM per device.

v0:
```python
import math
import jax
import jax.numpy as jnp
from jax import lax
from jax.sharding import PartitionSpec as P

D_LATENT = 256
ROPE = 64
NOPE = 128
VDIM = 128
MASKED = -1e30


def from_everyone(shard, axis):
    copies = jnp.broadcast_to(shard, (lax.axis_size(axis), *shard.shape))
    return lax.all_to_all(copies, axis, split_axis=0, concat_axis=0, tiled=True)


def joined_along(tiles, dim):
    tiles = jnp.moveaxis(tiles, 0, dim)
    dims = tiles.shape
    return tiles.reshape(*dims[:dim], dims[dim] * dims[dim + 1], *dims[dim + 2 :])


def gathered_copies(shard, axis, dim):
    tiles = from_everyone(shard, axis)
    return joined_along(tiles, dim)


def attend(state, key_block, key_start, setup):
    query_side, query_rope, query_pos, w_kv_up, absorb = setup
    numerator, running_max, totals = state
    key_count = key_block.shape[0]
    highest = lax.Precision.HIGHEST
    key_latent = key_block[:, :D_LATENT]
    key_rope = key_block[:, D_LATENT:]
    scores = jnp.einsum(
        "qhd,kd->hqk", query_side, key_latent.astype(jnp.float32), precision=highest
    )
    scores = scores + jnp.einsum(
        "qhd,kd->hqk", query_rope, key_rope, preferred_element_type=jnp.float32
    )
    scores = scores * (NOPE + ROPE) ** (-0.5)
    key_pos = key_start + lax.iota(jnp.int32, key_count)
    allowed = (key_pos[None, :] <= query_pos[:, None]) & (key_pos[None, :] >= 0)
    scores = jnp.where(allowed[None], scores, MASKED)
    new_max = jnp.maximum(running_max, jnp.max(scores, axis=2))
    factor = jnp.exp(running_max - new_max)
    weights = jnp.where(allowed[None], jnp.exp(scores - new_max[:, :, None]), 0.0)
    totals = totals * factor + jnp.sum(weights, axis=2)
    rounded = weights.astype(jnp.bfloat16)
    update = jnp.einsum("hqk,kd->hqd", rounded, key_latent, preferred_element_type=jnp.float32)
    numerator = numerator * factor[:, :, None] + update
    return (numerator, new_max, totals)


def attend_blocks(state, keys, setup):
    key_total = keys.shape[0]
    block_rows = math.gcd(key_total, 1024)
    block_count = key_total // block_rows

    def one_block(block_index, inner):
        offset = block_index * block_rows
        piece = lax.dynamic_slice_in_dim(keys, offset, block_rows, 0)
        return attend(inner, piece, offset, setup)

    return lax.fori_loop(0, block_count, one_block, state)


def prepare(query_rows, query_pos, w_kv_up):
    row_count = query_rows.shape[0]
    local_heads = w_kv_up.shape[1] // (NOPE + VDIM)
    query_all = query_rows.reshape(row_count, local_heads, NOPE + ROPE)
    w_key = w_kv_up.reshape(D_LATENT, local_heads, NOPE + VDIM)[:, :, :NOPE]
    query_side = jnp.einsum(
        "qhn,dhn->qhd", query_all[:, :, :NOPE], w_key, preferred_element_type=jnp.float32
    )
    width = D_LATENT
    setup = (query_side, query_all[:, :, NOPE:], query_pos, w_kv_up, True)
    start_state = (
        jnp.zeros((local_heads, row_count, width), jnp.float32),
        jnp.full((local_heads, row_count), MASKED, jnp.float32),
        jnp.zeros((local_heads, row_count), jnp.float32),
    )
    return (setup, start_state)


def finish(state, w_kv_up):
    numerator, running_max, totals = state
    local_heads = w_kv_up.shape[1] // (NOPE + VDIM)
    row_count = totals.shape[1]
    w_value = w_kv_up.reshape(D_LATENT, local_heads, NOPE + VDIM)[:, :, NOPE:].astype(jnp.float32)
    numerator = jnp.einsum("hqd,dhv->hqv", numerator, w_value, precision=lax.Precision.HIGHEST)
    result = numerator / totals[:, :, None]
    return (
        jnp.transpose(result, (1, 0, 2)).reshape(row_count, local_heads * VDIM).astype(jnp.bfloat16)
    )


def body(queries, latent, w_kv_up):
    group_rows = queries.shape[0]
    group_index = lax.axis_index("seq")
    query_pos = group_index * group_rows + lax.iota(jnp.int32, group_rows)
    setup, state = prepare(queries, query_pos, w_kv_up)
    gathered = gathered_copies(latent, "head", 0)
    state = attend_blocks(state, lax.all_gather(gathered, "seq", axis=0, tiled=True), setup)
    return finish(state, w_kv_up)


def solution(mesh):
    in_specs = (P("seq", "head"), P(("seq", "head"), None), P(None, "head"))
    out_specs = P("seq", "head")
    return jax.shard_map(body, mesh=mesh, in_specs=in_specs, out_specs=out_specs, check_vma=False)
```

profile of v0, /device:TPU:1, one launch (start us, length us, event | category | flops | bytes accessed | tf_op | source)
XLA Modules:
  0.0 202.9 jit_solution(14311295889934789337)
XLA Ops:
  7.3 9.4 %all_to_all.5 = bf16[4,32,320]{2,1,0:T(8,128)(2,1)} all-to-all(bf16[4,32,320]{2,1,0:T(8,128)(2,1)S(1)} %broadcast_in_dim.69), channel_id=1, replica_groups=mesh['seq'=128,'head'=4] {'head'}, dimensions={0} | all-to-all | bytes 163840 | tf_op jit(solution)/shard_map/all_to_all | solution.py:16
  19.2 93.8 %all-gather.2.cloned.1.call-done = bf16[16384,320]{1,0:T(8,128)(2,1)} async-done(((bf16[128,320]{1,0:T(8,128)(2,1)}), bf16[16384,320]{1,0:T(8,128)(2,1)}) %all-gather.2.cloned.1.call-update) | async-done | bytes 10485776 | tf_op jit(solution)/shard_map/all_gather | solution.py:106
  113.0 82.0 %while.18 = (s32[]{:T(128)}, f32[2,128,256]{2,1,0:T(8,128)S(1)}, f32[2,128]{1,0:T(2,128)S(1)}, f32[2,128]{1,0:T(2,128)S(1)}, bf16[16384,320]{1,0:T(8,128)(2,1)},...) while((s32[]{:T(128)}, f32[2,128,256]{2,1,0:T(8,128)S(1)}, ...), condition=%wide.region_3.4_spmd.clone, body=%wide.region_0.3_spmd.clone.sunk | while | flops 976163200 | bytes 7924967 | solution.py:67
  114.6 1.7 fusion.38
  119.7 1.7 fusion.38
  121.7 1.5 convolution_add_fusion.3
  124.8 1.7 fusion.38
  130.0 1.7 fusion.38
  135.1 1.7 fusion.38
  137.1 1.5 convolution_add_fusion.3
  140.2 1.7 fusion.38
  145.4 1.7 fusion.38
  150.5 1.7 fusion.38
  152.4 1.5 convolution_add_fusion.3
  155.6 1.7 fusion.38
  160.7 1.7 fusion.38
  165.9 1.7 fusion.38
  167.8 1.5 convolution_add_fusion.3
  171.0 1.7 fusion.38
  176.1 1.7 fusion.38
  181.2 1.7 fusion.38
  183.2 1.5 convolution_add_fusion.3
  186.4 1.7 fusion.38
  191.5 1.7 fusion.38
  (168 shorter events, 50.1 us)
Async XLA Ops:
  6.5 106.5 %all-gather.2.cloned.1.call-start = ((), (), s32[]{:S(2)}) async-start(), calls=%async_computation.1 | async-start | bytes 12681216 | tf_op jit(solution)/shard_map/all_gather | solution.py:106
Sparse Core Ops, SparseCore 0:
  16.8 96.1 all-gather.1
where the time goes:
time: 205 us; the launch traced here: 203 us
  waiting for transfers between devices  93.8 us (46%)
  matrix products  71.6 us (35%)
  between operations  13.5 us (7%)
  other arithmetic  9.62 us (5%)
  blocking collectives  9.39 us (5%)
  local copies, waits for them, and re-layouts  3.76 us (2%)
    all_gather x1, waiting for transfers between devices, body(): lax.all_gather(gathered, 'seq', axis=0, tiled=True)  93.8 us
    dot_general x16, matrix products, attend(): jnp.einsum('qhd,kd->hqk', query_side, key_latent.astype(jnp.float32), pre...  27.3 us
    dot_general x16, matrix products, attend(): jnp.einsum('hqk,kd->hqd', rounded, key_latent, preferred_element_type=jnp...  24.2 us
    dot_general x16, matrix products, attend(): jnp.einsum('qhd,kd->hqk', query_rope, key_rope, preferred_element_type=jn...  19.6 us
    all_to_all x1, blocking collectives, from_everyone(): return lax.all_to_all(copies, axis, split_axis=0, concat_axis=0, tiled=True)  9.39 us
    and x16, other arithmetic, attend(): allowed = (key_pos[None, :] <= query_pos[:, None]) & (key_pos[None, :] >= 0)  5.39 us
  transfers between devices with their start and end apart: 1, of which 1 were waited for; matrix products, arithmetic and copies ran while one was open for 1% of the time, Pallas kernels for 0%

commit v1 on v0

--- a/solution.py
+++ b/solution.py
@@ -1,3 +1,4 @@
+import functools
 import math
 import jax
 import jax.numpy as jnp
@@ -9,6 +10,16 @@
 NOPE = 128
 VDIM = 128
 MASKED = -1e30
+
+
+def trace_plate(q_in, along_dim):
+    local_now = lax.axis_size("seq")
+    aux = jnp.stack([q_in] * local_now, 0)
+    x_next = lax.all_to_all(aux, "seq", 0, 0)
+    return jnp.concatenate(x_next, along_dim)
+
+
+rings_rest = functools.partial(trace_plate, along_dim=0)
 
 
 def from_everyone(shard, axis):
@@ -103,7 +114,7 @@
     query_pos = group_index * group_rows + lax.iota(jnp.int32, group_rows)
     setup, state = prepare(queries, query_pos, w_kv_up)
     gathered = gathered_copies(latent, "head", 0)
-    state = attend_blocks(state, lax.all_gather(gathered, "seq", axis=0, tiled=True), setup)
+    state = attend_blocks(state, rings_rest(gathered), setup)
     return finish(state, w_kv_up)
 
 

time: 205 us -> 461 us (2.25)
  the two profiles are of different devices: /device:TPU:1 before, /device:TPU:105 now
where the time goes in v1:
time: 461 us; the launch traced here: 458 us
  waiting for transfers between devices  325 us (70%)
  matrix products  71.6 us (16%)
  local copies, waits for them, and re-layouts  23.6 us (5%)
  starting transfers between devices  18.7 us (4%)
  other arithmetic  9.62 us (2%)
  blocking collectives  8.47 us (2%)
    all_to_all x1, waiting for transfers between devices, trace_plate(): x_next = lax.all_to_all(aux, 'seq', 0, 0)  325 us
    dot_general x16, matrix products, attend(): jnp.einsum('qhd,kd->hqk', query_side, key_latent.astype(jnp.float32), pre...  27.3 us
    dot_general x16, matrix products, attend(): jnp.einsum('hqk,kd->hqd', rounded, key_latent, preferred_element_type=jnp...  24.3 us
    dot_general x16, matrix products, attend(): jnp.einsum('qhd,kd->hqk', query_rope, key_rope, preferred_element_type=jn...  19.5 us
    all_to_all x1, starting transfers between devices, trace_plate(): x_next = lax.all_to_all(aux, 'seq', 0, 0)  18.7 us
    unnamed x8, local copies, waits for them, and re-layouts  15.4 us
  transfers between devices with their start and end apart: 1, of which 1 were waited for; matrix products, arithmetic and copies ran while one was open for 0% of the time, Pallas kernels for 0%

profile of v1, /device:TPU:105, one launch (start us, length us, event | category | flops | bytes accessed | tf_op | source)
XLA Modules:
  0.0 458.5 jit_solution(10054707968017435752)
XLA Ops:
  0.7 8.5 %all_to_all.10 = bf16[4,32,320]{2,1,0:T(8,128)(2,1)S(1)} all-to-all(bf16[4,32,320]{2,1,0:T(8,128)(2,1)S(1)} %broadcast_in_dim.69), channel_id=1, replica_groups=mesh['seq'=128,'head'=4] {'head'}, dimensions={0} | all-to-all | bytes 163840 | tf_op jit(solution)/shard_map/all_to_all | solution.py:27
  9.3 6.6 %stack.3 = bf16[128,128,320]{1,2,0:T(8,128)(2,1)} broadcast(bf16[128,320]{0,1:T(8,128)(2,1)S(1)} %copy.29), dimensions={1,2} | broadcast | bytes 10567680 | tf_op jit(solution)/shard_map/stack | solution.py:17
  15.9 18.7 %all-to-all-start.1 = ((bf16[128,128,320]{1,2,0:T(8,128)(2,1)}), bf16[128,128,320]{1,2,0:T(8,128)(2,1)}, u32[]{:S(2)}, u32[]{:S(2)}) async-start(bf16[128,128,320]{1,2,0:T(8,128)(2,1)} %stack.3), calls=%async_computation.1 | async-start | bytes 20971520 | tf_op jit(solution)/shard_map/all_to_all | solution.py:18
  35.4 325.0 %all-to-all-done.1 = bf16[128,128,320]{1,2,0:T(8,128)(2,1)} async-done(((bf16[128,128,320]{1,2,0:T(8,128)(2,1)}), bf16[128,128,320]{1,2,0:T(8,128)(2,1)}, u32[]{:S(2)}, u32[]{:S(2)}) %all-to-all-start.1) | async-done | bytes 10485792 | tf_op jit(solution)/shard_map/all_to_all | solution.py:18
  360.4 15.0 %copy.40 = bf16[128,128,320]{2,1,0:T(8,128)(2,1)} copy(bf16[128,128,320]{1,2,0:T(8,128)(2,1)} %all-to-all-done.1) | data formatting | bytes 20971520
  375.4 82.0 %while.18 = (s32[]{:T(128)}, f32[2,128,256]{2,1,0:T(8,128)S(1)}, f32[2,128]{1,0:T(2,128)S(1)}, f32[2,128]{1,0:T(2,128)S(1)}, bf16[16384,320]{1,0:T(8,128)(2,1)},...) while((s32[]{:T(128)}, f32[2,128,256]{2,1,0:T(8,128)S(1)}, ...), condition=%wide.region_3.4_spmd.clone, body=%wide.region_0.3_spmd.clone.sunk | while | flops 976163200 | bytes 7924967 | solution.py:78
  377.0 1.7 fusion.38
  379.0 1.5 convolution_add_fusion.3
  382.1 1.7 fusion.38
  387.3 1.7 fusion.38
  392.4 1.7 fusion.38
  394.4 1.5 convolution_add_fusion.3
  397.5 1.7 fusion.38
  402.6 1.7 fusion.38
  407.8 1.7 fusion.38
  412.9 1.7 fusion.38
  418.0 1.7 fusion.38
  423.2 1.7 fusion.38
  428.3 1.7 fusion.38
  433.4 1.7 fusion.38
  438.5 1.7 fusion.38
  443.7 1.7 fusion.38
  448.8 1.7 fusion.38
  453.9 1.7 fusion.38
  (174 shorter events, 52.9 us)
Async XLA Ops:
  15.9 18.7 %copy-start = (bf16[256,512]{1,0:T(8,128)(2,1)S(1)}, bf16[256,512]{1,0:T(8,128)(2,1)}, u32[]{:S(2)}) copy-start(bf16[256,512]{1,0:T(8,128)(2,1)} %param.7) | copy-start | bytes 786436
  15.9 18.9 %copy-start.1 = (bf16[128,384]{1,0:T(8,128)(2,1)S(1)}, bf16[128,384]{1,0:T(8,128)(2,1)}, u32[]{:S(2)}) copy-start(bf16[128,384]{1,0:T(8,128)(2,1)} %param.5) | copy-start | bytes 294916
  15.9 344.5 %all-to-all-start.1 = ((bf16[128,128,320]{1,2,0:T(8,128)(2,1)}), bf16[128,128,320]{1,2,0:T(8,128)(2,1)}, u32[]{:S(2)}, u32[]{:S(2)}) async-start(bf16[128,128,320]{1,2,0:T(8,128)(2,1)} %stack.3), calls=%async_computation.1 | async-start | bytes 20971520 | tf_op jit(solution)/shard_map/all_to_all | solution.py:18
